TPU v7x, 32 devices: a whole 2x2x4 slice. The times are simulated.
32 devices in a mesh: node: 8 (over z, x), freq: 4 (over y, core).
Axes of the slice: x: 2, y: 2, z: 4, core: 2. Of those that a mesh axis runs over, the one named last changes fastest.
Arguments:
- action_old: float32 [36, 36, 4096], P('freq', None, 'node'), may hold values from 0.05 to 2
- source: float32 [36, 36, 4096], P('freq', None, 'node'), may hold values from -4 to 4
- time_weight: float32 [4096], P('node'), may hold values from 0.5 to 4
- group_speed: float32 [36], P('freq'), may hold values from 0.3 to 3
- normals: float32 [2, 8, 4096], P(None, None, 'node'), may hold values from -3 to 3
- refract: float32 [4096], P('node'), may hold values from -4 to 4
- freq_shift: float32 [4096], P('node'), may hold values from -4 to 4
- nbr_list: int32 [8, 6], P('node'), may hold values from -1 to 7, as said below
- send_nodes: int32 [8, 6, 32], P('node'), may hold values from 0 to 511, as said below
- adjacency: int32 [8, 4096], P(None, 'node'), may hold values from 0 to 703, as said below
Outputs:
- action_new: float32 [36, 36, 4096], P('freq', None, 'node')
Inputs may be any that keep to these rules, and one draw needn't show every extreme that they name: `nbr_list`: slot entries of subdomain p are distinct subdomains (p + o) or (p - o) modulo the number of subdomains, 1 <= o <= 3, or -1 for an empty slot; p + 1 and p - 1 are always listed; if p lists q then q lists p. `send_nodes`: local node indices of the sending subdomain. `adjacency`: entries as in the first step; an entry at or above 512 never names an empty slot.
All inputs are finite; a program needn't handle non-finite values.
Results may differ from a plain program's by a relative error of at most 0.000088.
Values sent between devices are 32-bit elements; how exact they have to be, the bound alone decides.
A program may use at most 128 MiB of HBM per device.

v0:
```python
import functools
import math

import jax
import jax.numpy as jnp
import numpy as np
from jax import lax
from jax.experimental import pallas as pl
from jax.experimental.pallas import tpu as pltpu
from jax.sharding import PartitionSpec as P

REACH = 3
ITERS = 3
MESH = pl.DeviceIdType.MESH
OFFSETS = [sign * reach for reach in range(1, REACH + 1) for sign in (1, -1)]


def ceil_to(value, unit):
    return -(-value // unit) * unit


def split(value):
    high = value.astype(jnp.bfloat16)
    low = (value - high.astype(jnp.float32)).astype(jnp.bfloat16)
    return high, low


def dot(a, b):
    return jnp.dot(a, b, preferred_element_type=jnp.float32)


def kernel(
    count,
    fcount,
    speed,
    nbrs,
    picks,
    adjacency,
    time_weight,
    refract,
    freq_shift,
    normals,
    trig,
    action_old,
    source,
    out,
    spectra,
    steady,
    inverse,
    weights,
    turns,
    pieces,
    pick_matrix,
    selector,
    halo_selector,
    halo_pieces,
    gathered,
    staged,
    parcels,
    landed,
    bands_landed,
    send_sems,
    recv_sems,
):
    bands, angles, local = action_old.shape
    padded = turns.shape[1]
    slots, width = picks.shape[1], picks.shape[2]
    degree = adjacency.shape[0]
    rows = bands * padded
    wide = landed.shape[2]
    halo = slots * width
    halo_wide = halo_selector.shape[1]
    me = lax.axis_index("node")
    fme = lax.axis_index("freq")
    targets = [lax.rem(me + o + count, count) for o in OFFSETS]
    anchors = [lax.rem(me - o + count, count) for o in OFFSETS]
    above = lax.rem(fme + 1, fcount)
    below = lax.rem(fme + fcount - 1, fcount)
    partners = [{"node": t} for t in targets] + [{"freq": above}, {"freq": below}]

    barrier = pltpu.get_barrier_semaphore()
    for partner in partners:
        pl.semaphore_signal(barrier, inc=1, device_id=partner, device_id_type=MESH)

    def block(f):
        return pl.ds(f * padded, padded)

    def copies(step):
        result = []
        for j in range(len(OFFSETS)):
            piece = pl.ds(j * width, width)
            result.append((parcels.at[step, piece], landed.at[step, piece]))
        result.append((spectra.at[step, block(bands - 1)], bands_landed.at[step, 0]))
        result.append((spectra.at[step, block(0)], bands_landed.at[step, 1]))
        return [
            pltpu.make_async_remote_copy(
                src_ref=src,
                dst_ref=dst,
                send_sem=send_sems.at[step, i],
                recv_sem=recv_sems.at[step, i],
                device_id=partners[i],
                device_id_type=MESH,
            )
            for i, (src, dst) in enumerate(result)
        ]

    def prepare(step):
        high, low = split(spectra[step])
        pieces[0] = high
        pieces[1] = low
        staged[pl.ds(0, rows)] = dot(pieces[0], pick_matrix[...]) + dot(
            pieces[1], pick_matrix[...]
        )
        parcels[step] = jnp.transpose(staged[...])[:halo]

    def put(step, f, value):
        base = f * padded
        spectra[step, pl.ds(base, angles)] = value
        spectra[step, pl.ds(base + angles, 1)] = value[:1]
        spectra[step, pl.ds(base + padded - 1, 1)] = value[angles - 1 : angles]

    spectra[...] = jnp.zeros_like(spectra)
    if wide > rows:
        staged[pl.ds(rows, wide - rows)] = jnp.zeros((wide - rows, halo_wide), jnp.float32)
    for f in range(bands):
        put(0, f, action_old[f])
    chosen = []
    for target in targets:
        row = jnp.full((1, width), -1, jnp.int32)
        for s in range(slots):
            hit = jnp.full((1, width), nbrs[0, s], jnp.int32) == target
            row = jnp.where(hit, picks[0, pl.ds(s, 1)], row)
        chosen.append(row)
    if halo_wide > halo:
        chosen.append(jnp.full((1, halo_wide - halo), -1, jnp.int32))
    chosen = jnp.concatenate(chosen, axis=1)
    node_ids = lax.broadcasted_iota(jnp.int32, (local, halo_wide), 0)
    pick_matrix[...] = jnp.where(node_ids == chosen, 1.0, 0.0).astype(jnp.bfloat16)
    prepare(0)
    pl.semaphore_wait(barrier, len(partners))
    flights = [copies(0)]
    for copy in flights[0]:
        copy.start()

    repeats = local // trig.shape[2]
    cosine = jnp.concatenate([trig[0]] * repeats, axis=1)
    sine = jnp.concatenate([trig[1]] * repeats, axis=1)
    weight = time_weight[...].reshape(1, local)
    shift = freq_shift[...].reshape(1, local)
    turning = refract[...].reshape(1, local) * cosine
    turns[0] = jnp.maximum(turning, 0.0)
    turns[1] = jnp.maximum(-turning, 0.0)
    own = lax.broadcasted_iota(jnp.int32, (1, local), 1)
    outflow = jnp.zeros((padded, local), jnp.float32)
    for k in range(degree):
        entry = adjacency[pl.ds(k, 1)]
        used = jnp.where(entry != own, 1.0, 0.0)
        flow = (cosine * normals[0, pl.ds(k, 1)] + sine * normals[1, pl.ds(k, 1)]) * used
        outflow = outflow + jnp.maximum(flow, 0.0)
        weights[k] = jnp.maximum(-flow, 0.0)
        moved = entry
        for s in range(slots):
            place = jnp.zeros_like(entry)
            for j, anchor in enumerate(anchors):
                hit = jnp.full((1, local), nbrs[0, s], jnp.int32) == anchor
                place = jnp.where(hit, (j - s) * width, place)
            first = local + s * width
            inside = (entry >= first) & (entry < first + width)
            moved = moved + jnp.where(inside, place, 0)
        ids = lax.broadcasted_iota(jnp.int32, (local, local), 0)
        selector[k] = jnp.where(ids == moved, 1.0, 0.0).astype(jnp.bfloat16)
        halo_ids = lax.broadcasted_iota(jnp.int32, (halo_wide, local), 0) + local
        halo_selector[k] = jnp.where(halo_ids == moved, 1.0, 0.0).astype(jnp.bfloat16)
    still = weight + jnp.abs(turning) + jnp.abs(shift)
    for f in range(bands):
        inverse[block(f)] = 1.0 / (still + speed[f] * outflow)
        steady[block(f)] = jnp.zeros((padded, local), jnp.float32)
        steady[pl.ds(f * padded, angles)] = weight * action_old[f] + source[f]
    rising = jnp.maximum(shift, 0.0)
    falling = jnp.maximum(-shift, 0.0)
    has_below = jnp.where(jnp.full((1, local), fme, jnp.int32) > 0, rising, 0.0)
    has_above = jnp.where(jnp.full((1, local), fme, jnp.int32) < fcount - 1, falling, 0.0)

    for step in range(ITERS):
        gathered[...] = jnp.zeros_like(gathered)

        def near(k, carry):
            found = dot(pieces[0], selector[k]) + dot(pieces[1], selector[k])
            for f in range(bands):
                gathered[block(f)] += weights[k] * found[f * padded : (f + 1) * padded]
            return carry

        lax.fori_loop(0, degree, near, 0)
        for copy in flights[step]:
            copy.wait_recv()
        received = landed[step]
        if halo_wide > halo:
            received = jnp.concatenate(
                [received, jnp.zeros((halo_wide - halo, wide), jnp.float32)], axis=0
            )
        high, low = split(jnp.transpose(received)[:rows])
        halo_pieces[0] = high
        halo_pieces[1] = low

        def far(k, carry):
            found = dot(halo_pieces[0], halo_selector[k]) + dot(halo_pieces[1], halo_selector[k])
            for f in range(bands):
                gathered[block(f)] += weights[k] * found[f * padded : (f + 1) * padded]
            return carry

        lax.fori_loop(0, degree, far, 0)
        for f in range(bands):
            here = spectra[step, block(f)]
            total = steady[block(f)] + speed[f] * gathered[block(f)]
            total = total + turns[0] * pltpu.roll(here, 1, 0)
            total = total + turns[1] * pltpu.roll(here, padded - 1, 0)
            if f > 0:
                total = total + rising * spectra[step, block(f - 1)]
            else:
                total = total + has_below * bands_landed[step, 0]
            if f < bands - 1:
                total = total + falling * spectra[step, block(f + 1)]
            else:
                total = total + has_above * bands_landed[step, 1]
            value = (total * inverse[block(f)])[:angles]
            if step < ITERS - 1:
                put(step + 1, f, value)
            else:
                out[f] = value
        if step < ITERS - 1:
            prepare(step + 1)
            flights.append(copies(step + 1))
            for copy in flights[step + 1]:
                copy.start()
    for flight in flights:
        for copy in flight:
            copy.wait_send()


def body(count, fcount, *args):
    (
        action_old,
        source,
        time_weight,
        group_speed,
        normals,
        refract,
        freq_shift,
        nbr_list,
        send_nodes,
        adjacency,
    ) = args
    bands, angles, local = action_old.shape
    slots, width = send_nodes.shape[1:]
    degree = adjacency.shape[0]
    padded = ceil_to(angles + 2, 8)
    rows = bands * padded
    wide = ceil_to(rows, 128)
    halo = slots * width
    halo_wide = ceil_to(halo, 128)
    theta = 2.0 * math.pi * (np.arange(padded) % angles) / angles
    trig = np.stack([np.cos(theta), np.sin(theta)]).astype(np.float32)
    trig = jnp.asarray(np.ascontiguousarray(np.broadcast_to(trig[:, :, None], (2, padded, 128))))
    vmem = pl.BlockSpec(memory_space=pltpu.VMEM)
    smem = pl.BlockSpec(memory_space=pltpu.SMEM)
    f32, bf16 = jnp.float32, jnp.bfloat16
    copies = len(OFFSETS) + 2
    return pl.pallas_call(
        functools.partial(kernel, count, fcount),
        out_shape=jax.ShapeDtypeStruct(action_old.shape, f32),
        in_specs=[smem, smem] + [vmem] * 9,
        out_specs=vmem,
        scratch_shapes=[
            pltpu.VMEM((ITERS, rows, local), f32),
            pltpu.VMEM((rows, local), f32),
            pltpu.VMEM((rows, local), f32),
            pltpu.VMEM((degree, padded, local), f32),
            pltpu.VMEM((2, padded, local), f32),
            pltpu.VMEM((2, rows, local), bf16),
            pltpu.VMEM((local, halo_wide), bf16),
            pltpu.VMEM((degree, local, local), bf16),
            pltpu.VMEM((degree, halo_wide, local), bf16),
            pltpu.VMEM((2, rows, halo_wide), bf16),
            pltpu.VMEM((rows, local), f32),
            pltpu.VMEM((wide, halo_wide), f32),
            pltpu.VMEM((ITERS, halo, wide), f32),
            pltpu.VMEM((ITERS, halo, wide), f32),
            pltpu.VMEM((ITERS, 2, padded, local), f32),
            pltpu.SemaphoreType.DMA((ITERS, copies)),
            pltpu.SemaphoreType.DMA((ITERS, copies)),
        ],
        compiler_params=pltpu.CompilerParams(
            collective_id=0, has_side_effects=True, vmem_limit_bytes=48 * 1024 * 1024
        ),
    )(
        group_speed,
        nbr_list,
        send_nodes,
        adjacency,
        time_weight,
        refract,
        freq_shift,
        normals,
        trig,
        action_old,
        source,
    )


def solution(mesh):
    in_specs = (
        P("freq", None, "node"),
        P("freq", None, "node"),
        P("node"),
        P("freq"),
        P(None, None, "node"),
        P("node"),
        P("node"),
        P("node", None),
        P("node", None, None),
        P(None, "node"),
    )
    return jax.shard_map(
        functools.partial(body, mesh.shape["node"], mesh.shape["freq"]),
        mesh=mesh,
        in_specs=in_specs,
        out_specs=P("freq", None, "node"),
        check_vma=False,
    )
```

profile of v0, /device:TPU:0, one launch (start us, length us, event | category | flops | bytes accessed | tf_op | source)
XLA Modules:
  0.0 45.7 jit_solution(12094625234737859415)
XLA Ops:
  0.0 0.0 copy-start.9
  0.0 0.0 copy-start.7
  0.0 0.0 copy-start.6
  0.0 0.0 copy-start.8
  0.0 0.0 copy-start.5
  0.0 0.8 %copy.12.picks = s32[1,6,32]{2,1,0:T(8,128)S(1)} copy(s32[1,6,32]{2,0,1:T(1,128)} %param.19) | data formatting | bytes 1536 | tf_op args[8]
  0.8 0.0 copy-done.9
  0.8 0.0 copy-done.7
  0.8 0.0 copy-done.6
  0.8 0.0 copy-done.8
  0.8 0.0 copy-done.5
  0.8 0.0 copy-start
  0.8 1.1 %copy-done = f32[9,36,512]{2,1,0:T(8,128)S(1)} copy-done((f32[9,36,512]{2,1,0:T(8,128)S(1)}, f32[9,36,512]{2,1,0:T(8,128)}, u32[]{:S(2)}) %copy-start) | copy-done | bytes 663576
  1.9 0.0 copy-start.1
  1.9 1.1 %copy-done.1 = f32[9,36,512]{2,1,0:T(8,128)S(1)} copy-done((f32[9,36,512]{2,1,0:T(8,128)S(1)}, f32[9,36,512]{2,1,0:T(8,128)}, u32[]{:S(2)}) %copy-start.1) | copy-done | bytes 663576
  3.0 0.0 copy-start.2
  3.0 0.8 %copy-done.2 = f32[2,40,128]{2,1,0:T(8,128)S(1)} copy-done((f32[2,40,128]{2,1,0:T(8,128)S(1)}, f32[2,40,128]{2,1,0:T(8,128)}, u32[]{:S(2)}) %copy-start.2) | copy-done | bytes 40984
  3.8 0.0 copy-start.3
  3.8 0.8 %copy-done.3 = f32[2,8,512]{2,1,0:T(8,128)S(1)} copy-done((f32[2,8,512]{2,1,0:T(8,128)S(1)}, f32[2,8,512]{2,1,0:T(8,128)}, u32[]{:S(2)}) %copy-start.3) | copy-done | bytes 32792
  4.6 0.0 copy-start.4
  4.6 0.7 %copy-done.4 = s32[8,512]{1,0:T(8,128)S(1)} copy-done((s32[8,512]{1,0:T(8,128)S(1)}, s32[8,512]{1,0:T(8,128)}, u32[]{:S(2)}) %copy-start.4) | copy-done | bytes 16408
  5.3 39.6 %shard_map.109 = f32[9,36,512]{2,1,0:T(8,128)S(1)} custom-call(f32[9]{0:T(128)S(1)} %copy-done.8, s32[1,6]{1,0:T(1,128)S(1)} %copy-done.9, s32[1,6,32]{2,1,0:T(8,128)S(1)} %copy.12.picks, s32[8,512]{1,0:T(8,128)S(1)} %copy-done.4, f32[512]{0:T(512)S(1)} %copy-done.5, f32[512]{0:T(512)S(1)} %copy-done.6, f32[512]{0:T(512)S(1)} %copy-done.7, ...), custom_call_target="tpu_custom_call" | custom-call | tf_op jit(solution)/shard_map/pallas_call | solution.py:268
  44.9 0.9 %copy.14 = f32[9,36,512]{2,1,0:T(8,128)} copy(f32[9,36,512]{2,1,0:T(8,128)S(1)} %shard_map.109) | data formatting | bytes 1327104
Async XLA Ops:
  0.0 0.8 %copy-start.9 = (s32[1,6]{1,0:T(1,128)S(1)}, s32[1,6]{1,0:T(1,128)}, u32[]{:S(2)}) copy-start(s32[1,6]{1,0:T(1,128)} %nbrs.1) | copy-start | bytes 76
  0.0 0.8 %copy-start.7 = (f32[512]{0:T(512)S(1)}, f32[512]{0:T(512)}, u32[]{:S(2)}) copy-start(f32[512]{0:T(512)} %freq_shift.1) | copy-start | bytes 6148
  0.0 0.8 %copy-start.6 = (f32[512]{0:T(512)S(1)}, f32[512]{0:T(512)}, u32[]{:S(2)}) copy-start(f32[512]{0:T(512)} %refract.1) | copy-start | bytes 6148
  0.0 0.8 %copy-start.8 = (f32[9]{0:T(128)S(1)}, f32[9]{0:T(128)}, u32[]{:S(2)}) copy-start(f32[9]{0:T(128)} %speed.1) | copy-start | bytes 112
  0.0 0.8 %copy-start.5 = (f32[512]{0:T(512)S(1)}, f32[512]{0:T(512)}, u32[]{:S(2)}) copy-start(f32[512]{0:T(512)} %time_weight.1) | copy-start | bytes 6148
  0.8 1.1 %copy-start = (f32[9,36,512]{2,1,0:T(8,128)S(1)}, f32[9,36,512]{2,1,0:T(8,128)}, u32[]{:S(2)}) copy-start(f32[9,36,512]{2,1,0:T(8,128)} %action_old.1) | copy-start | bytes 1990660
  1.9 1.1 %copy-start.1 = (f32[9,36,512]{2,1,0:T(8,128)S(1)}, f32[9,36,512]{2,1,0:T(8,128)}, u32[]{:S(2)}) copy-start(f32[9,36,512]{2,1,0:T(8,128)} %source.1) | copy-start | bytes 1990660
  3.0 0.8 %copy-start.2 = (f32[2,40,128]{2,1,0:T(8,128)S(1)}, f32[2,40,128]{2,1,0:T(8,128)}, u32[]{:S(2)}) copy-start(f32[2,40,128]{2,1,0:T(8,128)} %constant.2.clone.trig) | copy-start | bytes 122884
  3.8 0.8 %copy-start.3 = (f32[2,8,512]{2,1,0:T(8,128)S(1)}, f32[2,8,512]{2,1,0:T(8,128)}, u32[]{:S(2)}) copy-start(f32[2,8,512]{2,1,0:T(8,128)} %normals.1) | copy-start | bytes 98308
  4.6 0.7 %copy-start.4 = (s32[8,512]{1,0:T(8,128)S(1)}, s32[8,512]{1,0:T(8,128)}, u32[]{:S(2)}) copy-start(s32[8,512]{1,0:T(8,128)} %adjacency.1) | copy-start | bytes 49156
where the time goes:
time: 46.2 us; the launch traced here: 45.7 us
  Pallas kernels  39.6 us (86%)
  local copies, waits for them, and re-layouts  6.11 us (13%)
    pallas_call x1, Pallas kernels, body(): pl.pallas_call(functools.partial(kernel, count, fcount), out_shape=jax.Sh...  39.6 us
    unnamed x22, local copies, waits for them, and re-layouts  6.11 us

commit v1 on v0

v1 whole, which is shorter than its diff:
```python
import functools
import math

import jax
import jax.numpy as jnp
import numpy as np
from jax import lax
from jax.experimental import pallas as pl
from jax.experimental.pallas import tpu as pltpu
from jax.sharding import PartitionSpec as P

REACH = 3
ITERS = 3
CHUNKS = (2, 1)
UNROLL = 4
SEND_ORDER = (4, 5, 0, 1, 2, 3)
MESH = pl.DeviceIdType.MESH
OFFSETS = [sign * reach for reach in range(1, REACH + 1) for sign in (1, -1)]


def ceil_to(value, unit):
    return -(-value // unit) * unit


def split(value):
    high = value.astype(jnp.bfloat16)
    low = (value - high.astype(jnp.float32)).astype(jnp.bfloat16)
    return high, low


def dot(a, b):
    return jnp.dot(a, b, preferred_element_type=jnp.float32)


def kernel(
    count,
    fcount,
    speed_hbm,
    nbrs_hbm,
    picks_hbm,
    adjacency_hbm,
    time_weight_hbm,
    refract_hbm,
    freq_shift_hbm,
    normals_hbm,
    trig_hbm,
    action_hbm,
    source_hbm,
    out,
    speed,
    nbrs,
    picks,
    adjacency,
    time_weight,
    refract,
    freq_shift,
    normals,
    trig,
    action_old,
    source,
    load_sems,
    spectra,
    steady,
    inverse,
    weights,
    turns,
    pieces,
    pick_matrix,
    selector,
    halo_selector,
    halo_pieces,
    gathered,
    parcels,
    landed,
    bands_landed,
    send_sems,
    recv_sems,
):
    bands, angles, local = action_old.shape
    padded = turns.shape[1]
    slots, width = picks.shape[0], picks.shape[2]
    degree = adjacency.shape[0]
    rows = bands * padded
    wide = landed.shape[2]
    halo = slots * width
    halo_wide = halo_selector.shape[1]
    me = lax.axis_index("node")
    fme = lax.axis_index("freq")
    targets = [lax.rem(me + o + count, count) for o in OFFSETS]
    anchors = [lax.rem(me - o + count, count) for o in OFFSETS]
    above = lax.rem(fme + 1, fcount)
    below = lax.rem(fme + fcount - 1, fcount)
    partners = [{"node": t} for t in targets] + [{"freq": above}, {"freq": below}]

    barrier = pltpu.get_barrier_semaphore()
    for partner in partners:
        pl.semaphore_signal(barrier, inc=1, device_id=partner, device_id_type=MESH)

    names = [
        (action_hbm, action_old),
        (nbrs_hbm, nbrs),
        (picks_hbm, picks),
        (adjacency_hbm, adjacency),
        (normals_hbm, normals),
        (trig_hbm, trig),
        (refract_hbm, refract),
        (time_weight_hbm, time_weight),
        (freq_shift_hbm, freq_shift),
        (speed_hbm, speed),
        (source_hbm, source),
    ]
    loads = [pltpu.make_async_copy(a, b, load_sems.at[i]) for i, (a, b) in enumerate(names)]
    for load in loads:
        load.start()

    def neighbour(s, lanes):
        return jnp.broadcast_to(nbrs[:, s : s + 1], (1, lanes))

    def block(f):
        return pl.ds(f * padded, padded)

    group = 128 // padded
    used_rows = group * padded
    bounds = [sum(CHUNKS[:c]) for c in range(len(CHUNKS) + 1)]
    flights = {}

    def send(step, i, src, dst, partner):
        copy = pltpu.make_async_remote_copy(
            src_ref=src,
            dst_ref=dst,
            send_sem=send_sems.at[step, i],
            recv_sem=recv_sems.at[step, i],
            device_id=partners[partner],
            device_id_type=MESH,
        )
        copy.start()
        flights[step, i] = copy

    def send_chunk(step, c):
        lanes = pl.ds(bounds[c] * 128, CHUNKS[c] * 128)
        for j in SEND_ORDER:
            piece = (step, pl.ds(j * width, width), lanes)
            send(step, c * len(OFFSETS) + j, parcels.at[piece], landed.at[piece], j)

    def send_band(step, up):
        i = len(OFFSETS) * len(CHUNKS) + up
        src = spectra.at[step, block(bands - 1 if up else 0)]
        send(step, i, src, bands_landed.at[step, 1 - up], len(OFFSETS) + 1 - up)

    def prepare(step, c):
        rows_c = pl.ds(bounds[c] * used_rows, CHUNKS[c] * used_rows)
        high, low = split(spectra[step, rows_c])
        pieces[0, rows_c] = high
        pieces[1, rows_c] = low
        found = dot(high, pick_matrix[...]) + dot(low, pick_matrix[...])
        for g in range(CHUNKS[c]):
            part = found[g * used_rows : (g + 1) * used_rows]
            if used_rows < 128:
                fill = jnp.zeros((128 - used_rows, halo_wide), jnp.float32)
                part = jnp.concatenate([part, fill], axis=0)
            lanes = pl.ds((bounds[c] + g) * 128, 128)
            parcels[step, :, lanes] = jnp.transpose(part)[:halo]

    def put(step, f, value):
        base = f * padded
        spectra[step, pl.ds(base, angles)] = value
        spectra[step, pl.ds(base + angles, 1)] = value[:1]
        spectra[step, pl.ds(base + padded - 1, 1)] = value[angles - 1 : angles]

    spectra[...] = jnp.zeros_like(spectra)
    loads[0].wait()
    for f in range(bands):
        put(0, f, action_old[f])
    for load in loads[1:3]:
        load.wait()
    chosen = []
    for target in targets:
        row = jnp.full((1, width), -1, jnp.int32)
        for s in range(slots):
            hit = neighbour(s, width) == target
            row = jnp.where(hit, picks[s], row)
        chosen.append(row)
    if halo_wide > halo:
        chosen.append(jnp.full((1, halo_wide - halo), -1, jnp.int32))
    chosen = jnp.concatenate(chosen, axis=1)
    node_ids = lax.broadcasted_iota(jnp.int32, (local, halo_wide), 0)
    pick_matrix[...] = jnp.where(node_ids == chosen, 1.0, 0.0).astype(jnp.bfloat16)
    for c in range(len(CHUNKS)):
        prepare(0, c)
    for load in loads[3:]:
        load.wait()

    repeats = local // trig.shape[2]
    cosine = jnp.concatenate([trig[0]] * repeats, axis=1)
    sine = jnp.concatenate([trig[1]] * repeats, axis=1)
    weight = time_weight[...].reshape(1, local)
    shift = freq_shift[...].reshape(1, local)
    turning = refract[...].reshape(1, local) * cosine
    turns[0] = jnp.maximum(turning, 0.0)
    turns[1] = jnp.maximum(-turning, 0.0)
    own = lax.broadcasted_iota(jnp.int32, (1, local), 1)
    outflow = jnp.zeros((padded, local), jnp.float32)
    for k in range(degree):
        entry = adjacency[pl.ds(k, 1)]
        used = jnp.where(entry != own, 1.0, 0.0)
        flow = (cosine * normals[0, pl.ds(k, 1)] + sine * normals[1, pl.ds(k, 1)]) * used
        outflow = outflow + jnp.maximum(flow, 0.0)
        weights[k] = jnp.maximum(-flow, 0.0)
        moved = entry
        for s in range(slots):
            place = jnp.zeros_like(entry)
            for j, anchor in enumerate(anchors):
                hit = neighbour(s, local) == anchor
                place = jnp.where(hit, (j - s) * width, place)
            first = local + s * width
            inside = (entry >= first) & (entry < first + width)
            moved = moved + jnp.where(inside, place, 0)
        ids = lax.broadcasted_iota(jnp.int32, (local, local), 0)
        selector[k] = jnp.where(ids == moved, 1.0, 0.0).astype(jnp.bfloat16)
        halo_ids = lax.broadcasted_iota(jnp.int32, (halo_wide, local), 0) + local
        halo_selector[k] = jnp.where(halo_ids == moved, 1.0, 0.0).astype(jnp.bfloat16)
    still = weight + jnp.abs(turning) + jnp.abs(shift)
    speeds = speed[...].reshape(1, bands)
    gain = [jnp.broadcast_to(speeds[:, f : f + 1], (1, local)) for f in range(bands)]
    for f in range(bands):
        inverse[block(f)] = 1.0 / (still + gain[f] * outflow)
        steady[block(f)] = jnp.zeros((padded, local), jnp.float32)
        steady[pl.ds(f * padded, angles)] = weight * action_old[f] + source[f]
    rising = jnp.maximum(shift, 0.0)
    falling = jnp.maximum(-shift, 0.0)
    has_below = jnp.where(jnp.full((1, local), fme, jnp.int32) > 0, rising, 0.0)
    has_above = jnp.where(jnp.full((1, local), fme, jnp.int32) < fcount - 1, falling, 0.0)

    pl.semaphore_wait(barrier, len(partners))
    for c in range(len(CHUNKS)):
        send_chunk(0, c)
    send_band(0, 0)
    send_band(0, 1)

    for step in range(ITERS):
        gathered[...] = jnp.zeros_like(gathered)

        def near(i, carry):
            for u in range(UNROLL):
                k = i * UNROLL + u
                found = dot(pieces[0], selector[k]) + dot(pieces[1], selector[k])
                for f in range(bands):
                    gathered[block(f)] += weights[k] * found[f * padded : (f + 1) * padded]
            return carry

        lax.fori_loop(0, degree // UNROLL, near, 0)
        for c in range(len(CHUNKS)):
            for j in range(len(OFFSETS)):
                flights[step, c * len(OFFSETS) + j].wait_recv()
            base = bounds[c] * used_rows
            count_c = CHUNKS[c] * used_rows
            fs = range(bounds[c] * group, (bounds[c] + CHUNKS[c]) * group)
            for g in range(bounds[c], bounds[c + 1]):
                received = landed[step, :, pl.ds(g * 128, 128)]
                if halo_wide > halo:
                    fill = jnp.zeros((halo_wide - halo, 128), jnp.float32)
                    received = jnp.concatenate([received, fill], axis=0)
                high, low = split(jnp.transpose(received)[:used_rows])
                halo_pieces[0, pl.ds(g * used_rows, used_rows)] = high
                halo_pieces[1, pl.ds(g * used_rows, used_rows)] = low

            def far(i, carry):
                for u in range(UNROLL):
                    k = i * UNROLL + u
                    found = dot(halo_pieces[0, pl.ds(base, count_c)], halo_selector[k])
                    found += dot(halo_pieces[1, pl.ds(base, count_c)], halo_selector[k])
                    for n, f in enumerate(fs):
                        part = found[n * padded : (n + 1) * padded]
                        gathered[block(f)] += weights[k] * part
                return carry

            lax.fori_loop(0, degree // UNROLL, far, 0)
            if 0 in fs:
                flights[step, len(OFFSETS) * len(CHUNKS) + 1].wait_recv()
            if bands - 1 in fs:
                flights[step, len(OFFSETS) * len(CHUNKS)].wait_recv()
            for f in fs:
                here = spectra[step, block(f)]
                total = steady[block(f)] + gain[f] * gathered[block(f)]
                total = total + turns[0] * pltpu.roll(here, 1, 0)
                total = total + turns[1] * pltpu.roll(here, padded - 1, 0)
                if f > 0:
                    total = total + rising * spectra[step, block(f - 1)]
                else:
                    total = total + has_below * bands_landed[step, 0]
                if f < bands - 1:
                    total = total + falling * spectra[step, block(f + 1)]
                else:
                    total = total + has_above * bands_landed[step, 1]
                value = (total * inverse[block(f)])[:angles]
                if step < ITERS - 1:
                    put(step + 1, f, value)
                else:
                    out[f] = value
            if step < ITERS - 1:
                prepare(step + 1, c)
                send_chunk(step + 1, c)
                if 0 in fs:
                    send_band(step + 1, 0)
                if bands - 1 in fs:
                    send_band(step + 1, 1)
    for flight in flights.values():
        flight.wait_send()


def body(count, fcount, *args):
    (
        action_old,
        source,
        time_weight,
        group_speed,
        normals,
        refract,
        freq_shift,
        nbr_list,
        send_nodes,
        adjacency,
    ) = args
    bands, angles, local = action_old.shape
    slots, width = send_nodes.shape[1:]
    send_nodes = jnp.transpose(send_nodes, (1, 0, 2))
    degree = adjacency.shape[0]
    padded = ceil_to(angles + 2, 8)
    rows = bands * padded
    wide = sum(CHUNKS) * 128
    halo = slots * width
    halo_wide = ceil_to(halo, 128)
    theta = 2.0 * math.pi * (np.arange(padded) % angles) / angles
    trig = np.stack([np.cos(theta), np.sin(theta)]).astype(np.float32)
    trig = jnp.asarray(np.ascontiguousarray(np.broadcast_to(trig[:, :, None], (2, padded, 128))))
    vmem = pl.BlockSpec(memory_space=pltpu.VMEM)
    hbm = pl.BlockSpec(memory_space=pltpu.HBM)
    f32, bf16 = jnp.float32, jnp.bfloat16
    copies = len(OFFSETS) * len(CHUNKS) + 2
    assert (sum(CHUNKS) * (128 // padded), degree % UNROLL) == (bands, 0)
    operands = (
        group_speed,
        nbr_list,
        send_nodes,
        adjacency,
        time_weight,
        refract,
        freq_shift,
        normals,
        trig,
        action_old,
        source,
    )
    return pl.pallas_call(
        functools.partial(kernel, count, fcount),
        out_shape=jax.ShapeDtypeStruct(action_old.shape, f32),
        in_specs=[hbm] * len(operands),
        out_specs=vmem,
        scratch_shapes=[pltpu.VMEM(x.shape, x.dtype) for x in operands]
        + [
            pltpu.SemaphoreType.DMA((len(operands),)),
            pltpu.VMEM((ITERS, rows, local), f32),
            pltpu.VMEM((rows, local), f32),
            pltpu.VMEM((rows, local), f32),
            pltpu.VMEM((degree, padded, local), f32),
            pltpu.VMEM((2, padded, local), f32),
            pltpu.VMEM((2, rows, local), bf16),
            pltpu.VMEM((local, halo_wide), bf16),
            pltpu.VMEM((degree, local, local), bf16),
            pltpu.VMEM((degree, halo_wide, local), bf16),
            pltpu.VMEM((2, rows, halo_wide), bf16),
            pltpu.VMEM((rows, local), f32),
            pltpu.VMEM((ITERS, halo, wide), f32),
            pltpu.VMEM((ITERS, halo, wide), f32),
            pltpu.VMEM((ITERS, 2, padded, local), f32),
            pltpu.SemaphoreType.DMA((ITERS, copies)),
            pltpu.SemaphoreType.DMA((ITERS, copies)),
        ],
        compiler_params=pltpu.CompilerParams(
            collective_id=0, has_side_effects=True, vmem_limit_bytes=48 * 1024 * 1024
        ),
    )(*operands)


def solution(mesh):
    in_specs = (
        P("freq", None, "node"),
        P("freq", None, "node"),
        P("node"),
        P("freq"),
        P(None, None, "node"),
        P("node"),
        P("node"),
        P("node", None),
        P("node", None, None),
        P(None, "node"),
    )
    return jax.shard_map(
        functools.partial(body, mesh.shape["node"], mesh.shape["freq"]),
        mesh=mesh,
        in_specs=in_specs,
        out_specs=P("freq", None, "node"),
        check_vma=False,
    )
```

time: 46.2 us -> 42.9 us (0.929)
  Pallas kernels: 39.6 us -> 33.7 us
  local copies, waits for them, and re-layouts: 6.11 us -> 8.74 us
    pallas_call x1, Pallas kernels: 39.6 us -> 33.7 us  [body(): pl.pallas_call(functools.partial(kernel, count, fcount), out_shape=jax.Sh...]
    unnamed x22 -> x23, local copies, waits for them, and re-layouts: 6.11 us -> 8.74 us
where the time goes in v1:
time: 42.9 us; the launch traced here: 42.4 us
  Pallas kernels  33.7 us (79%)
  local copies, waits for them, and re-layouts  8.74 us (20%)
    pallas_call x1, Pallas kernels, body(): pl.pallas_call(functools.partial(kernel, count, fcount), out_shape=jax.Sh...  33.7 us
    unnamed x23, local copies, waits for them, and re-layouts  8.74 us

profile of v1, /device:TPU:0, one launch (start us, length us, event | category | flops | bytes accessed | tf_op | source)
XLA Modules:
  0.0 42.4 jit_solution(1537583519587981700)
XLA Ops:
  0.0 0.0 copy-start.10
  0.0 0.0 copy-start.9
  0.0 0.7 %copy-done.10 = s32[1,6]{1,0:T(1,128)S(1)} copy-done((s32[1,6]{1,0:T(1,128)S(1)}, s32[1,6]{1,0:T(1,128)}, u32[]{:S(2)}) %copy-start.10) | copy-done | bytes 48
  0.7 0.0 copy-done.9
  0.7 0.0 copy-start
  0.7 1.1 %copy-done = f32[9,36,512]{2,1,0:T(8,128)S(1)} copy-done((f32[9,36,512]{2,1,0:T(8,128)S(1)}, f32[9,36,512]{2,1,0:T(8,128)}, u32[]{:S(2)}) %copy-start) | copy-done | bytes 663576
  1.8 0.0 copy-start.1
  1.8 1.1 %copy-done.1 = f32[9,36,512]{2,1,0:T(8,128)S(1)} copy-done((f32[9,36,512]{2,1,0:T(8,128)S(1)}, f32[9,36,512]{2,1,0:T(8,128)}, u32[]{:S(2)}) %copy-start.1) | copy-done | bytes 663576
  2.9 0.0 copy-start.2
  2.9 0.8 %copy-done.2 = f32[2,40,128]{2,1,0:T(8,128)S(1)} copy-done((f32[2,40,128]{2,1,0:T(8,128)S(1)}, f32[2,40,128]{2,1,0:T(8,128)}, u32[]{:S(2)}) %copy-start.2) | copy-done | bytes 40984
  3.7 0.0 copy-start.3
  3.7 0.8 %copy-done.3 = f32[2,8,512]{2,1,0:T(8,128)S(1)} copy-done((f32[2,8,512]{2,1,0:T(8,128)S(1)}, f32[2,8,512]{2,1,0:T(8,128)}, u32[]{:S(2)}) %copy-start.3) | copy-done | bytes 32792
  4.4 0.0 copy-start.4
  4.4 0.7 %copy-done.4 = s32[8,512]{1,0:T(8,128)S(1)} copy-done((s32[8,512]{1,0:T(8,128)S(1)}, s32[8,512]{1,0:T(8,128)}, u32[]{:S(2)}) %copy-start.4) | copy-done | bytes 16408
  5.2 0.0 copy-start.5
  5.2 0.7 %copy-done.5 = s32[1,6,32]{2,0,1:T(1,128)S(1)} copy-done((s32[1,6,32]{2,0,1:T(1,128)S(1)}, s32[1,6,32]{2,0,1:T(1,128)}, u32[]{:S(2)}) %copy-start.5) | copy-done | bytes 792
  5.8 0.0 copy-start.6
  5.8 0.7 %copy-done.6 = f32[512]{0:T(512)S(1)} copy-done((f32[512]{0:T(512)S(1)}, f32[512]{0:T(512)}, u32[]{:S(2)}) %copy-start.6) | copy-done | bytes 2072
  6.5 0.0 copy-start.7
  6.5 0.7 %copy-done.7 = f32[512]{0:T(512)S(1)} copy-done((f32[512]{0:T(512)S(1)}, f32[512]{0:T(512)}, u32[]{:S(2)}) %copy-start.7) | copy-done | bytes 2072
  7.2 0.0 copy-start.8
  7.2 0.7 %copy-done.8 = f32[512]{0:T(512)S(1)} copy-done((f32[512]{0:T(512)S(1)}, f32[512]{0:T(512)}, u32[]{:S(2)}) %copy-start.8) | copy-done | bytes 2072
  7.9 33.7 %shard_map.109 = f32[9,36,512]{2,1,0:T(8,128)S(1)} custom-call(f32[9]{0:T(128)S(1)} %copy-done.9, s32[1,6]{1,0:T(1,128)S(1)} %copy-done.10, s32[6,1,32]{2,1,0:T(1,128)S(1)} %bitcast.1, s32[8,512]{1,0:T(8,128)S(1)} %copy-done.4, f32[512]{0:T(512)S(1)} %copy-done.6, f32[512]{0:T(512)S(1)} %copy-done.7, f32[512]{0:T(512)S(1)} %copy-done.8, ...), custom_call_target="tpu_custom_call" | custom-call | tf_op jit(solution)/shard_map/pallas_call | solution.py:354
  41.6 0.9 %copy.13 = f32[9,36,512]{2,1,0:T(8,128)} copy(f32[9,36,512]{2,1,0:T(8,128)S(1)} %shard_map.109) | data formatting | bytes 1327104
Async XLA Ops:
  0.0 0.7 %copy-start.10 = (s32[1,6]{1,0:T(1,128)S(1)}, s32[1,6]{1,0:T(1,128)}, u32[]{:S(2)}) copy-start(s32[1,6]{1,0:T(1,128)} %nbrs_hbm.1) | copy-start | bytes 76
  0.0 0.7 %copy-start.9 = (f32[9]{0:T(128)S(1)}, f32[9]{0:T(128)}, u32[]{:S(2)}) copy-start(f32[9]{0:T(128)} %speed_hbm.1) | copy-start | bytes 112
  0.7 1.1 %copy-start = (f32[9,36,512]{2,1,0:T(8,128)S(1)}, f32[9,36,512]{2,1,0:T(8,128)}, u32[]{:S(2)}) copy-start(f32[9,36,512]{2,1,0:T(8,128)} %action_hbm.1) | copy-start | bytes 1990660
  1.8 1.1 %copy-start.1 = (f32[9,36,512]{2,1,0:T(8,128)S(1)}, f32[9,36,512]{2,1,0:T(8,128)}, u32[]{:S(2)}) copy-start(f32[9,36,512]{2,1,0:T(8,128)} %source_hbm.1) | copy-start | bytes 1990660
  2.9 0.8 %copy-start.2 = (f32[2,40,128]{2,1,0:T(8,128)S(1)}, f32[2,40,128]{2,1,0:T(8,128)}, u32[]{:S(2)}) copy-start(f32[2,40,128]{2,1,0:T(8,128)} %constant.2.clone.trig_hbm) | copy-start | bytes 122884
  3.7 0.8 %copy-start.3 = (f32[2,8,512]{2,1,0:T(8,128)S(1)}, f32[2,8,512]{2,1,0:T(8,128)}, u32[]{:S(2)}) copy-start(f32[2,8,512]{2,1,0:T(8,128)} %normals_hbm.1) | copy-start | bytes 98308
  4.4 0.7 %copy-start.4 = (s32[8,512]{1,0:T(8,128)S(1)}, s32[8,512]{1,0:T(8,128)}, u32[]{:S(2)}) copy-start(s32[8,512]{1,0:T(8,128)} %adjacency_hbm.1) | copy-start | bytes 49156
  5.2 0.7 %copy-start.5 = (s32[1,6,32]{2,0,1:T(1,128)S(1)}, s32[1,6,32]{2,0,1:T(1,128)}, u32[]{:S(2)}) copy-start(s32[1,6,32]{2,0,1:T(1,128)} %param.19) | copy-start | bytes 2308
  5.8 0.7 %copy-start.6 = (f32[512]{0:T(512)S(1)}, f32[512]{0:T(512)}, u32[]{:S(2)}) copy-start(f32[512]{0:T(512)} %time_weight_hbm.1) | copy-start | bytes 6148
  6.5 0.7 %copy-start.7 = (f32[512]{0:T(512)S(1)}, f32[512]{0:T(512)}, u32[]{:S(2)}) copy-start(f32[512]{0:T(512)} %refract_hbm.1) | copy-start | bytes 6148
  7.2 0.7 %copy-start.8 = (f32[512]{0:T(512)S(1)}, f32[512]{0:T(512)}, u32[]{:S(2)}) copy-start(f32[512]{0:T(512)} %freq_shift_hbm.1) | copy-start | bytes 6148
